TPU v7x, 32 devices: a whole 2x2x4 slice. The times are simulated.
32 devices in a mesh: band: 4 (over y, x), grid: 8 (over z, core).
Axes of the slice: x: 2, y: 2, z: 4, core: 2. Of those that a mesh axis runs over, the one named last changes fastest.
Arguments:
- wavefunctions: bfloat16 [1024, 131072], P('band', 'grid'), may hold values from -6 to 6
- projectors: bfloat16 [512, 8, 13, 256], P('grid'), may hold values from -0.0068359375 to 0.0068359375
- slot_atom: int32 [512, 8], P('grid'), may hold values from -1 to 255, as said below
- occupations: float32 [1024], P('band'), may hold values from 0.02 to 2
Outputs:
- density: float32 [256, 13, 13], P('grid')
Inputs may be any that keep to these rules, and one draw needn't show every extreme that they name: `slot_atom`: -1 marks an empty slot. Any other entry is an atom a whose owning domain a // 32 lies within 3 domains, counted around the closed cycle of 8 domains, of the domain of the block, block index // 64. In every domain some block has all 8 slots filled.
All inputs are finite; a program needn't handle non-finite values.
Results may differ from a plain program's by a relative error of at most 0.0003.
Values sent between devices are 32-bit elements; how exact they have to be, the bound alone decides.
A program may use at most 64 MiB of HBM per device.

v0:
```python
import jax
import jax.numpy as jnp
from jax import lax
from jax.sharding import PartitionSpec as P

REACH = 3
ATOMS_DEV = 32


def shifted(block, axis, distance):
    devices = range(lax.axis_size(axis))
    route = [((i - distance) % len(devices), i) for i in devices]
    return lax.ppermute(block, axis, route)


def body(wavefunctions, projectors, slot_atom, occupations):
    band_count = wavefunctions.shape[0]
    block_count, capacity, proj_count, block_len = projectors.shape
    domains = lax.axis_size("grid")
    domain = lax.axis_index("grid")
    window_len = 2 * REACH + 1
    row_len = proj_count * band_count
    grid_blocks = wavefunctions.reshape(band_count, block_count, block_len)
    stacked = projectors.reshape(block_count, capacity * proj_count, block_len)
    slot_terms = jnp.einsum(
        "ngb,gcb->gcn", grid_blocks, stacked, preferred_element_type=jnp.float32
    )
    slot_terms = slot_terms.reshape(block_count * capacity, row_len)
    slot_ids = slot_atom.reshape(-1)
    owner = jnp.floor_divide(slot_ids, ATOMS_DEV)
    offset = jnp.mod(owner - domain + REACH, domains)
    target = jnp.where(
        slot_ids >= 0, offset * ATOMS_DEV + jnp.mod(slot_ids, ATOMS_DEV), window_len * ATOMS_DEV
    )
    selector = (
        jnp.arange(window_len * ATOMS_DEV, dtype=jnp.int32)[:, None] == target[None, :]
    ).astype(jnp.float32)
    window = jnp.dot(
        selector, slot_terms, precision=lax.Precision.HIGHEST, preferred_element_type=jnp.float32
    )
    window = window.reshape(window_len, ATOMS_DEV, row_len)
    forward = window[2 * REACH]
    for hop in range(REACH, 0, -1):
        forward = shifted(forward, "grid", 1) + window[REACH + hop - 1]
    backward = window[0]
    for hop in range(REACH, 0, -1):
        addend = window[REACH - hop + 1] if hop > 1 else jnp.zeros_like(backward)
        backward = shifted(backward, "grid", -1) + addend
    owned = forward + backward
    owned = owned.reshape(ATOMS_DEV, proj_count, band_count)
    weighted = owned * occupations.reshape(1, 1, band_count)
    partial_sum = jnp.einsum("ain,ajn->aij", weighted, owned, precision=lax.Precision.HIGHEST)
    density = lax.psum(partial_sum, "band")
    return density


def solution(mesh):
    in_specs = (P("band", "grid"), P("grid", None, None, None), P("grid", None), P("band"))
    out_specs = P("grid", None, None)
    return jax.shard_map(body, mesh=mesh, in_specs=in_specs, out_specs=out_specs, check_vma=False)
```

profile of v0, /device:TPU:0, one launch (start us, length us, event | category | flops | bytes accessed | tf_op | source)
XLA Modules:
  0.0 87.4 jit_solution(6354588679132287062)
XLA Ops:
  0.0 2.8 %copy.8 = bf16[64,8,13,256]{3,0,2,1:T(8,128)(2,1)S(1)} copy(bf16[64,8,13,256]{3,1,2,0:T(8,128)(2,1)} %param.5) | data formatting | bytes 6815744 | tf_op args[1]
  2.8 9.4 %fusion = f32[64,104,256]{2,1,0:T(8,128)} fusion(bf16[32,64,8,256]{3,2,1,0:T(8,128)(2,1)} %bitcast.8, bf16[64,104,256]{2,0,1:T(8,128)(2,1)S(1)} %bitcast.7), kind=kOutput, calls=%fused_computation | convolution fusion | flops 872415232 | bytes 18612224 | tf_op jit(solution)/shard_map/ngb,gcb->gcn/dot_general | solution.py:25
  12.2 8.5 %reshape.103 = f32[512,3328]{1,0:T(8,128)} reshape(f32[64,104,256]{2,1,0:T(8,128)} %fusion) | data formatting | bytes 13631488 | tf_op jit(solution)/shard_map/reshape | solution.py:28
  20.7 0.1 copy.7
  20.7 0.1 reshape.100
  20.9 6.3 %fusion.6 = f32[224,3328]{1,0:T(8,128)S(1)} fusion(f32[512,3328]{1,0:T(8,128)} %reshape.103, s32[512]{0:T(512)S(1)} %fusion.15), kind=kOutput, calls=%fused_computation.7 | convolution fusion | flops 4580294656 | bytes 9799680 | tf_op jit(solution)/shard_map/dot_general | solution.py:38
  27.2 0.5 collective-permute-start
  27.8 4.1 %collective-permute-start.3 = (f32[32,3328]{1,0:T(8,128)S(1)}, f32[32,3328]{1,0:T(8,128)S(1)}, u32[]{:S(2)}, u32[]{:S(2)}) collective-permute-start(f32[32,3328]{1,0:T(8,128)S(1)} %get-tuple-element.10), channel_id=1, source_target_pairs={{1,0},{2,1},{3,2},{4,3},{5,4},{6,5},{7,6},{0,7},{9,8},{10,9},{11,1... | collective-permute-start | bytes 1277960 | tf_op jit(solution)/shard_map/ppermute | solution.py:13
  31.9 7.7 %collective-permute-done = f32[32,3328]{1,0:T(8,128)S(1)} collective-permute-done((f32[32,3328]{1,0:T(8,128)S(1)}, f32[32,3328]{1,0:T(8,128)S(1)}, u32[]{:S(2)}, u32[]{:S(2)}) %collective-permute-start) | collective-permute-done | bytes 426016 | tf_op jit(solution)/shard_map/ppermute | solution.py:13
  39.6 0.4 collective-permute-done.3
  40.0 0.1 slice_add_fusion.4
  40.1 2.0 %collective-permute-start.1 = (f32[32,3328]{1,0:T(8,128)S(1)}, f32[32,3328]{1,0:T(8,128)S(1)}, u32[]{:S(2)}, u32[]{:S(2)}) collective-permute-start(f32[32,3328]{1,0:T(8,128)S(1)} %get-tuple-element.7), channel_id=1, source_target_pairs={{7,0},{0,1},{1,2},{2,3},{3,4},{4,5},{5,6},{6,7},{15,8},{8,9},{9,10... | collective-permute-start | bytes 1277960 | tf_op jit(solution)/shard_map/ppermute | solution.py:13
  42.1 1.8 %collective-permute-start.4 = (f32[32,3328]{1,0:T(8,128)S(1)}, f32[32,3328]{1,0:T(8,128)S(1)}, u32[]{:S(2)}, u32[]{:S(2)}) collective-permute-start(f32[32,3328]{1,0:T(8,128)S(1)} %get-tuple-element.8), channel_id=1, source_target_pairs={{1,0},{2,1},{3,2},{4,3},{5,4},{6,5},{7,6},{0,7},{9,8},{10,9},{11,1... | collective-permute-start | bytes 1277960 | tf_op jit(solution)/shard_map/ppermute | solution.py:13
  44.0 7.6 %collective-permute-done.1 = f32[32,3328]{1,0:T(8,128)S(1)} collective-permute-done((f32[32,3328]{1,0:T(8,128)S(1)}, f32[32,3328]{1,0:T(8,128)S(1)}, u32[]{:S(2)}, u32[]{:S(2)}) %collective-permute-start.1) | collective-permute-done | bytes 426016 | tf_op jit(solution)/shard_map/ppermute | solution.py:13
  51.5 0.2 collective-permute-done.4
  51.7 0.1 slice_add_fusion.3
  51.8 2.5 %collective-permute-start.2 = (f32[32,3328]{1,0:T(8,128)S(1)}, f32[32,3328]{1,0:T(8,128)S(1)}, u32[]{:S(2)}, u32[]{:S(2)}) collective-permute-start(f32[32,3328]{1,0:T(8,128)S(1)} %get-tuple-element.5), channel_id=1, source_target_pairs={{7,0},{0,1},{1,2},{2,3},{3,4},{4,5},{5,6},{6,7},{15,8},{8,9},{9,10... | collective-permute-start | bytes 1277960 | tf_op jit(solution)/shard_map/ppermute | solution.py:13
  54.2 1.4 %collective-permute-start.5 = (f32[32,3328]{1,0:T(8,128)S(1)}, f32[32,3328]{1,0:T(8,128)S(1)}, u32[]{:S(2)}, u32[]{:S(2)}) collective-permute-start(f32[32,3328]{1,0:T(8,128)S(1)} %get-tuple-element.6), channel_id=1, source_target_pairs={{1,0},{2,1},{3,2},{4,3},{5,4},{6,5},{7,6},{0,7},{9,8},{10,9},{11,1... | collective-permute-start | bytes 1277960 | tf_op jit(solution)/shard_map/ppermute | solution.py:13
  55.7 7.1 %collective-permute-done.2 = f32[32,3328]{1,0:T(8,128)S(1)} collective-permute-done((f32[32,3328]{1,0:T(8,128)S(1)}, f32[32,3328]{1,0:T(8,128)S(1)}, u32[]{:S(2)}, u32[]{:S(2)}) %collective-permute-start.2) | collective-permute-done | bytes 426016 | tf_op jit(solution)/shard_map/ppermute | solution.py:13
  62.8 1.0 %collective-permute-done.5 = f32[32,3328]{1,0:T(8,128)S(1)} collective-permute-done((f32[32,3328]{1,0:T(8,128)S(1)}, f32[32,3328]{1,0:T(8,128)S(1)}, u32[]{:S(2)}, u32[]{:S(2)}) %collective-permute-start.5) | collective-permute-done | bytes 426016 | tf_op jit(solution)/shard_map/ppermute | solution.py:13
  63.9 0.1 reshape.104
  64.0 0.6 fusion.4
  64.7 21.9 %psum.7 = f32[32,13,13]{2,1,0:T(8,128)S(1)} all-reduce(f32[32,13,13]{2,1,0:T(8,128)S(1)} %fusion.4), channel_id=1, replica_groups=mesh['band'=4,'grid'=8] {'band'}, use_global_device_ids=true, to_apply=%region_0.1 | all-reduce | flops 5408 | bytes 43264 | tf_op jit(solution)/shard_map/psum | solution.py:53
  86.6 0.8 copy.11
  (7 shorter events, 0.1 us)
Async XLA Ops:
  12.2 8.5 %copy-start = (s32[64,8]{0,1:T(8,128)S(1)}, s32[64,8]{0,1:T(8,128)}, u32[]{:S(2)}) copy-start(s32[64,8]{0,1:T(8,128)} %param.6) | copy-start | bytes 6148
  27.2 12.3 %collective-permute-start = (f32[32,3328]{1,0:T(8,128)S(1)}, f32[32,3328]{1,0:T(8,128)S(1)}, u32[]{:S(2)}, u32[]{:S(2)}) collective-permute-start(f32[32,3328]{1,0:T(8,128)S(1)} %get-tuple-element.9), channel_id=1, source_target_pairs={{7,0},{0,1},{1,2},{2,3},{3,4},{4,5},{5,6},{6,7},{15,8},{8,9},{9,10... | collective-permute-start | bytes 1277960 | tf_op jit(solution)/shard_map/ppermute | solution.py:13
  27.8 36.3 %copy-start.1 = (f32[256]{0:T(256)S(1)}, f32[256]{0:T(256)}, u32[]{:S(2)}) copy-start(f32[256]{0:T(256)} %param.7) | copy-start | bytes 3076
  27.8 12.2 %collective-permute-start.3 = (f32[32,3328]{1,0:T(8,128)S(1)}, f32[32,3328]{1,0:T(8,128)S(1)}, u32[]{:S(2)}, u32[]{:S(2)}) collective-permute-start(f32[32,3328]{1,0:T(8,128)S(1)} %get-tuple-element.10), channel_id=1, source_target_pairs={{1,0},{2,1},{3,2},{4,3},{5,4},{6,5},{7,6},{0,7},{9,8},{10,9},{11,1... | collective-permute-start | bytes 1277960 | tf_op jit(solution)/shard_map/ppermute | solution.py:13
  40.1 11.5 %collective-permute-start.1 = (f32[32,3328]{1,0:T(8,128)S(1)}, f32[32,3328]{1,0:T(8,128)S(1)}, u32[]{:S(2)}, u32[]{:S(2)}) collective-permute-start(f32[32,3328]{1,0:T(8,128)S(1)} %get-tuple-element.7), channel_id=1, source_target_pairs={{7,0},{0,1},{1,2},{2,3},{3,4},{4,5},{5,6},{6,7},{15,8},{8,9},{9,10... | collective-permute-start | bytes 1277960 | tf_op jit(solution)/shard_map/ppermute | solution.py:13
  42.1 9.6 %collective-permute-start.4 = (f32[32,3328]{1,0:T(8,128)S(1)}, f32[32,3328]{1,0:T(8,128)S(1)}, u32[]{:S(2)}, u32[]{:S(2)}) collective-permute-start(f32[32,3328]{1,0:T(8,128)S(1)} %get-tuple-element.8), channel_id=1, source_target_pairs={{1,0},{2,1},{3,2},{4,3},{5,4},{6,5},{7,6},{0,7},{9,8},{10,9},{11,1... | collective-permute-start | bytes 1277960 | tf_op jit(solution)/shard_map/ppermute | solution.py:13
  51.8 11.0 %collective-permute-start.2 = (f32[32,3328]{1,0:T(8,128)S(1)}, f32[32,3328]{1,0:T(8,128)S(1)}, u32[]{:S(2)}, u32[]{:S(2)}) collective-permute-start(f32[32,3328]{1,0:T(8,128)S(1)} %get-tuple-element.5), channel_id=1, source_target_pairs={{7,0},{0,1},{1,2},{2,3},{3,4},{4,5},{5,6},{6,7},{15,8},{8,9},{9,10... | collective-permute-start | bytes 1277960 | tf_op jit(solution)/shard_map/ppermute | solution.py:13
  54.2 9.6 %collective-permute-start.5 = (f32[32,3328]{1,0:T(8,128)S(1)}, f32[32,3328]{1,0:T(8,128)S(1)}, u32[]{:S(2)}, u32[]{:S(2)}) collective-permute-start(f32[32,3328]{1,0:T(8,128)S(1)} %get-tuple-element.6), channel_id=1, source_target_pairs={{1,0},{2,1},{3,2},{4,3},{5,4},{6,5},{7,6},{0,7},{9,8},{10,9},{11,1... | collective-permute-start | bytes 1277960 | tf_op jit(solution)/shard_map/ppermute | solution.py:13
where the time goes:
time: 87.8 us; the launch traced here: 87.4 us
  waiting for transfers between devices  24 us (27%)
  blocking collectives  21.9 us (25%)
  matrix products  16.3 us (19%)
  local copies, waits for them, and re-layouts  12.4 us (14%)
  starting transfers between devices  12.4 us (14%)
    ppermute x6, waiting for transfers between devices, shifted(): return lax.ppermute(block, axis, route)  24 us
    psum x1, blocking collectives, body(): density = lax.psum(partial_sum, 'band')  21.9 us
    ppermute x6, starting transfers between devices, shifted(): return lax.ppermute(block, axis, route)  12.4 us
    dot_general x1, matrix products, body(): jnp.einsum('ngb,gcb->gcn', grid_blocks, stacked, preferred_element_type=j...  9.38 us
    reshape x1, local copies, waits for them, and re-layouts, body(): slot_terms = slot_terms.reshape(block_count * capacity, row_len)  8.49 us
    dot_general x1, matrix products, body(): jnp.dot(selector, slot_terms, precision=lax.Precision.HIGHEST, preferred_...  6.29 us
    unnamed x6, local copies, waits for them, and re-layouts  2.86 us
  transfers between devices with their start and end apart: 6, of which 6 were waited for; matrix products, arithmetic and copies ran while one was open for 0% of the time, Pallas kernels for 0%

commit v1 on v0

--- a/solution.py
+++ b/solution.py
@@ -50,7 +50,8 @@
     owned = owned.reshape(ATOMS_DEV, proj_count, band_count)
     weighted = owned * occupations.reshape(1, 1, band_count)
     partial_sum = jnp.einsum("ain,ajn->aij", weighted, owned, precision=lax.Precision.HIGHEST)
-    density = lax.psum(partial_sum, "band")
+    pieces = lax.all_gather(partial_sum, "band", axis=0, tiled=False)
+    density = pieces.sum(axis=0)
     return density
 
 

time: 87.8 us -> 81.2 us (0.925)
  blocking collectives: 21.9 us -> 15.2 us
    psum x1 -> x0, blocking collectives: 21.9 us -> none  [body(): density = lax.psum(partial_sum, 'band')]
    all_gather x0 -> x1, blocking collectives: none -> 15.2 us  [body(): pieces = lax.all_gather(partial_sum, 'band', axis=0, tiled=False)]
where the time goes in v1:
time: 81.2 us; the launch traced here: 80.8 us
  waiting for transfers between devices  24 us (30%)
  matrix products  16.3 us (20%)
  blocking collectives  15.2 us (19%)
  local copies, waits for them, and re-layouts  12.4 us (15%)
  starting transfers between devices  12.4 us (15%)
    ppermute x6, waiting for transfers between devices, shifted(): return lax.ppermute(block, axis, route)  24 us
    all_gather x1, blocking collectives, body(): pieces = lax.all_gather(partial_sum, 'band', axis=0, tiled=False)  15.2 us
    ppermute x6, starting transfers between devices, shifted(): return lax.ppermute(block, axis, route)  12.4 us
    dot_general x1, matrix products, body(): jnp.einsum('ngb,gcb->gcn', grid_blocks, stacked, preferred_element_type=j...  9.38 us
    reshape x1, local copies, waits for them, and re-layouts, body(): slot_terms = slot_terms.reshape(block_count * capacity, row_len)  8.49 us
    dot_general x1, matrix products, body(): jnp.dot(selector, slot_terms, precision=lax.Precision.HIGHEST, preferred_...  6.29 us
    unnamed x6, local copies, waits for them, and re-layouts  2.86 us
  transfers between devices with their start and end apart: 6, of which 6 were waited for; matrix products, arithmetic and copies ran while one was open for 0% of the time, Pallas kernels for 0%

profile of v1, /device:TPU:0, one launch (start us, length us, event | category | flops | bytes accessed | tf_op | source)
XLA Modules:
  0.0 80.8 jit_solution(10281824514119819824)
XLA Ops:
  0.0 2.8 %copy.11 = bf16[64,8,13,256]{3,0,2,1:T(8,128)(2,1)S(1)} copy(bf16[64,8,13,256]{3,1,2,0:T(8,128)(2,1)} %param.5) | data formatting | bytes 6815744 | tf_op args[1]
  2.8 9.4 %fusion = f32[64,104,256]{2,1,0:T(8,128)} fusion(bf16[32,64,8,256]{3,2,1,0:T(8,128)(2,1)} %bitcast.9, bf16[64,104,256]{2,0,1:T(8,128)(2,1)S(1)} %bitcast.8), kind=kOutput, calls=%fused_computation | convolution fusion | flops 872415232 | bytes 18612224 | tf_op jit(solution)/shard_map/ngb,gcb->gcn/dot_general | solution.py:25
  12.2 8.5 %reshape.103 = f32[512,3328]{1,0:T(8,128)} reshape(f32[64,104,256]{2,1,0:T(8,128)} %fusion) | data formatting | bytes 13631488 | tf_op jit(solution)/shard_map/reshape | solution.py:28
  20.7 0.1 reshape.100
  20.9 6.3 %fusion.6 = f32[224,3328]{1,0:T(8,128)S(1)} fusion(f32[512,3328]{1,0:T(8,128)} %reshape.103, s32[512]{0:T(512)S(1)} %fusion.15), kind=kOutput, calls=%fused_computation.7 | convolution fusion | flops 4580294656 | bytes 9799680 | tf_op jit(solution)/shard_map/dot_general | solution.py:38
  27.2 0.5 collective-permute-start
  27.8 4.1 %collective-permute-start.3 = (f32[32,3328]{1,0:T(8,128)S(1)}, f32[32,3328]{1,0:T(8,128)S(1)}, u32[]{:S(2)}, u32[]{:S(2)}) collective-permute-start(f32[32,3328]{1,0:T(8,128)S(1)} %get-tuple-element.10), channel_id=1, source_target_pairs={{1,0},{2,1},{3,2},{4,3},{5,4},{6,5},{7,6},{0,7},{9,8},{10,9},{11,1... | collective-permute-start | bytes 1277960 | tf_op jit(solution)/shard_map/ppermute | solution.py:13
  31.9 7.7 %collective-permute-done = f32[32,3328]{1,0:T(8,128)S(1)} collective-permute-done((f32[32,3328]{1,0:T(8,128)S(1)}, f32[32,3328]{1,0:T(8,128)S(1)}, u32[]{:S(2)}, u32[]{:S(2)}) %collective-permute-start) | collective-permute-done | bytes 426016 | tf_op jit(solution)/shard_map/ppermute | solution.py:13
  39.6 0.4 collective-permute-done.3
  40.0 0.1 slice_add_fusion.4
  40.1 2.0 %collective-permute-start.1 = (f32[32,3328]{1,0:T(8,128)S(1)}, f32[32,3328]{1,0:T(8,128)S(1)}, u32[]{:S(2)}, u32[]{:S(2)}) collective-permute-start(f32[32,3328]{1,0:T(8,128)S(1)} %get-tuple-element.7), channel_id=1, source_target_pairs={{7,0},{0,1},{1,2},{2,3},{3,4},{4,5},{5,6},{6,7},{15,8},{8,9},{9,10... | collective-permute-start | bytes 1277960 | tf_op jit(solution)/shard_map/ppermute | solution.py:13
  42.1 1.8 %collective-permute-start.4 = (f32[32,3328]{1,0:T(8,128)S(1)}, f32[32,3328]{1,0:T(8,128)S(1)}, u32[]{:S(2)}, u32[]{:S(2)}) collective-permute-start(f32[32,3328]{1,0:T(8,128)S(1)} %get-tuple-element.8), channel_id=1, source_target_pairs={{1,0},{2,1},{3,2},{4,3},{5,4},{6,5},{7,6},{0,7},{9,8},{10,9},{11,1... | collective-permute-start | bytes 1277960 | tf_op jit(solution)/shard_map/ppermute | solution.py:13
  44.0 7.6 %collective-permute-done.1 = f32[32,3328]{1,0:T(8,128)S(1)} collective-permute-done((f32[32,3328]{1,0:T(8,128)S(1)}, f32[32,3328]{1,0:T(8,128)S(1)}, u32[]{:S(2)}, u32[]{:S(2)}) %collective-permute-start.1) | collective-permute-done | bytes 426016 | tf_op jit(solution)/shard_map/ppermute | solution.py:13
  51.5 0.2 collective-permute-done.4
  51.7 0.1 slice_add_fusion.3
  51.8 2.5 %collective-permute-start.2 = (f32[32,3328]{1,0:T(8,128)S(1)}, f32[32,3328]{1,0:T(8,128)S(1)}, u32[]{:S(2)}, u32[]{:S(2)}) collective-permute-start(f32[32,3328]{1,0:T(8,128)S(1)} %get-tuple-element.5), channel_id=1, source_target_pairs={{7,0},{0,1},{1,2},{2,3},{3,4},{4,5},{5,6},{6,7},{15,8},{8,9},{9,10... | collective-permute-start | bytes 1277960 | tf_op jit(solution)/shard_map/ppermute | solution.py:13
  54.2 1.4 %collective-permute-start.5 = (f32[32,3328]{1,0:T(8,128)S(1)}, f32[32,3328]{1,0:T(8,128)S(1)}, u32[]{:S(2)}, u32[]{:S(2)}) collective-permute-start(f32[32,3328]{1,0:T(8,128)S(1)} %get-tuple-element.6), channel_id=1, source_target_pairs={{1,0},{2,1},{3,2},{4,3},{5,4},{6,5},{7,6},{0,7},{9,8},{10,9},{11,1... | collective-permute-start | bytes 1277960 | tf_op jit(solution)/shard_map/ppermute | solution.py:13
  55.7 7.1 %collective-permute-done.2 = f32[32,3328]{1,0:T(8,128)S(1)} collective-permute-done((f32[32,3328]{1,0:T(8,128)S(1)}, f32[32,3328]{1,0:T(8,128)S(1)}, u32[]{:S(2)}, u32[]{:S(2)}) %collective-permute-start.2) | collective-permute-done | bytes 426016 | tf_op jit(solution)/shard_map/ppermute | solution.py:13
  62.8 1.0 %collective-permute-done.5 = f32[32,3328]{1,0:T(8,128)S(1)} collective-permute-done((f32[32,3328]{1,0:T(8,128)S(1)}, f32[32,3328]{1,0:T(8,128)S(1)}, u32[]{:S(2)}, u32[]{:S(2)}) %collective-permute-start.5) | collective-permute-done | bytes 426016 | tf_op jit(solution)/shard_map/ppermute | solution.py:13
  63.9 0.1 reshape.104
  64.0 0.6 fusion.4
  64.7 15.2 %all-gather = f32[128,13,13]{2,1,0:T(8,128)S(1)} all-gather(f32[32,13,13]{2,1,0:T(8,128)S(1)} %fusion.4), channel_id=2, replica_groups=mesh['band'=4,'grid'=8] {'band'}, dimensions={0}, use_global_device_ids=true | all-gather | bytes 108160 | tf_op jit(solution)/shard_map/all_gather | solution.py:53
  79.9 0.1 reduce_sum.9
  80.0 0.8 %copy.14 = f32[32,13,13]{0,2,1:T(8,128)} copy(f32[32,13,13]{2,1,0:T(8,128)S(1)} %reduce_sum.9) | data formatting | bytes 43264 | tf_op jit(solution)/shard_map/reduce_sum | solution.py:54
  (8 shorter events, 0.2 us)
Async XLA Ops:
  12.2 8.5 %copy-start = (s32[64,8]{0,1:T(8,128)S(1)}, s32[64,8]{0,1:T(8,128)}, u32[]{:S(2)}) copy-start(s32[64,8]{0,1:T(8,128)} %param.6) | copy-start | bytes 6148
  27.2 12.3 %collective-permute-start = (f32[32,3328]{1,0:T(8,128)S(1)}, f32[32,3328]{1,0:T(8,128)S(1)}, u32[]{:S(2)}, u32[]{:S(2)}) collective-permute-start(f32[32,3328]{1,0:T(8,128)S(1)} %get-tuple-element.9), channel_id=1, source_target_pairs={{7,0},{0,1},{1,2},{2,3},{3,4},{4,5},{5,6},{6,7},{15,8},{8,9},{9,10... | collective-permute-start | bytes 1277960 | tf_op jit(solution)/shard_map/ppermute | solution.py:13
  27.8 36.3 %copy-start.1 = (f32[256]{0:T(256)S(1)}, f32[256]{0:T(256)}, u32[]{:S(2)}) copy-start(f32[256]{0:T(256)} %param.7) | copy-start | bytes 3076
  27.8 12.2 %collective-permute-start.3 = (f32[32,3328]{1,0:T(8,128)S(1)}, f32[32,3328]{1,0:T(8,128)S(1)}, u32[]{:S(2)}, u32[]{:S(2)}) collective-permute-start(f32[32,3328]{1,0:T(8,128)S(1)} %get-tuple-element.10), channel_id=1, source_target_pairs={{1,0},{2,1},{3,2},{4,3},{5,4},{6,5},{7,6},{0,7},{9,8},{10,9},{11,1... | collective-permute-start | bytes 1277960 | tf_op jit(solution)/shard_map/ppermute | solution.py:13
  40.1 11.5 %collective-permute-start.1 = (f32[32,3328]{1,0:T(8,128)S(1)}, f32[32,3328]{1,0:T(8,128)S(1)}, u32[]{:S(2)}, u32[]{:S(2)}) collective-permute-start(f32[32,3328]{1,0:T(8,128)S(1)} %get-tuple-element.7), channel_id=1, source_target_pairs={{7,0},{0,1},{1,2},{2,3},{3,4},{4,5},{5,6},{6,7},{15,8},{8,9},{9,10... | collective-permute-start | bytes 1277960 | tf_op jit(solution)/shard_map/ppermute | solution.py:13
  42.1 9.6 %collective-permute-start.4 = (f32[32,3328]{1,0:T(8,128)S(1)}, f32[32,3328]{1,0:T(8,128)S(1)}, u32[]{:S(2)}, u32[]{:S(2)}) collective-permute-start(f32[32,3328]{1,0:T(8,128)S(1)} %get-tuple-element.8), channel_id=1, source_target_pairs={{1,0},{2,1},{3,2},{4,3},{5,4},{6,5},{7,6},{0,7},{9,8},{10,9},{11,1... | collective-permute-start | bytes 1277960 | tf_op jit(solution)/shard_map/ppermute | solution.py:13
  51.8 11.0 %collective-permute-start.2 = (f32[32,3328]{1,0:T(8,128)S(1)}, f32[32,3328]{1,0:T(8,128)S(1)}, u32[]{:S(2)}, u32[]{:S(2)}) collective-permute-start(f32[32,3328]{1,0:T(8,128)S(1)} %get-tuple-element.5), channel_id=1, source_target_pairs={{7,0},{0,1},{1,2},{2,3},{3,4},{4,5},{5,6},{6,7},{15,8},{8,9},{9,10... | collective-permute-start | bytes 1277960 | tf_op jit(solution)/shard_map/ppermute | solution.py:13
  54.2 9.6 %collective-permute-start.5 = (f32[32,3328]{1,0:T(8,128)S(1)}, f32[32,3328]{1,0:T(8,128)S(1)}, u32[]{:S(2)}, u32[]{:S(2)}) collective-permute-start(f32[32,3328]{1,0:T(8,128)S(1)} %get-tuple-element.6), channel_id=1, source_target_pairs={{1,0},{2,1},{3,2},{4,3},{5,4},{6,5},{7,6},{0,7},{9,8},{10,9},{11,1... | collective-permute-start | bytes 1277960 | tf_op jit(solution)/shard_map/ppermute | solution.py:13
